TPU v7x, 32 devices: a whole 2x2x4 slice. The times are simulated.
32 devices in a mesh: grid: 8 (over y, x, core), band: 4 (over z).
Axes of the slice: x: 2, y: 2, z: 4, core: 2. Of those that a mesh axis runs over, the one named last changes fastest.
Arguments:
- start: float32 [1, 4, 1, 64, 32768], P(None, None, None, 'band', 'grid'), may hold values from -6 to 6
- energies: float32 [4, 64, 32768], P(None, 'band', 'grid'), may hold values from -4 to 4
- sites: int32 [3, 1], replicated, may hold values from 0 to 31
- potential: float32 [32, 32, 32], replicated, may hold values from -4 to 400
Outputs:
- alphas: float32 [1, 1, 4], replicated
- betas: float32 [1, 1, 4], replicated
- lanczos: float32 [1, 4, 1, 64, 32768], P(None, None, None, 'band', 'grid')
All inputs are finite; a program needn't handle non-finite values.
Results may differ from a plain program's by a relative error of at most 0.0003.
Values sent between devices are 32-bit elements; how exact they have to be, the bound alone decides.
A program may use at most 64 MiB of HBM per device.

v0:
```python
import math

import jax
import jax.numpy as jnp
from jax import lax
from jax.sharding import PartitionSpec as P

ITERS = 4


precise_mode = lax.Precision.HIGHEST


def cas_table(grid_size):
    cells = jnp.arange(grid_size, dtype=jnp.int32)
    phase = cells[:, None] * cells[None, :] % grid_size
    angle = phase.astype(jnp.float32) * (2.0 * math.pi / grid_size)
    return jnp.cos(angle) + jnp.sin(angle)


def shift_axis(field_part, offset, axis_number):
    length = field_part.shape[axis_number]
    doubled = jnp.concatenate([field_part, field_part], axis=axis_number)
    first_index = (length - offset) % length
    return lax.dynamic_slice_in_dim(doubled, first_index, length, axis_number)


def expand_coef(values):
    return values[:, None, :, None, None]


def body(start, energies, sites, potential):
    grid_size = potential.shape[0]
    volume = grid_size * grid_size * grid_size
    atom_count, core_count, pol_count, band_local, kpoint_local = start.shape
    plane_count = grid_size // lax.axis_size("grid")
    position = lax.axis_index("grid")
    chain_count = core_count * pol_count * band_local
    field_count = atom_count * chain_count
    total_count = (
        core_count * band_local * lax.axis_size("band") * kpoint_local * lax.axis_size("grid")
    )
    cas_grid = cas_table(grid_size)
    shifted = shift_axis(potential, sites[0, 0], 0)
    shifted = shift_axis(shifted, sites[1, 0], 1)
    shifted = shift_axis(shifted, sites[2, 0], 2)
    tables = [shifted]
    shifted_all = jnp.stack(tables, axis=-1)
    slab_table = lax.dynamic_slice_in_dim(shifted_all, position * plane_count, plane_count, 1)

    def moment(left, right):
        return jnp.sum(left * right, axis=(1, 3, 4)) / total_count

    start_sum = lax.psum(moment(start, start), ("grid", "band"))
    lanczos = start / expand_coef(jnp.sqrt(start_sum))
    previous = jnp.zeros_like(start)
    beta_prev = jnp.zeros((atom_count, pol_count), jnp.float32)
    alpha_list = []
    beta_list = []
    for iteration in range(ITERS):
        spread_fields = lanczos.reshape(atom_count, chain_count, plane_count, grid_size, grid_size)
        spread_over_z = jnp.einsum(
            "arpyz,wz->pywar", spread_fields, cas_grid, precision=precise_mode
        )
        spread_over_y = jnp.einsum(
            "pywar,uy->puwar", spread_over_z, cas_grid, precision=precise_mode
        )
        direct_spectrum = lax.all_to_all(
            spread_over_y.reshape(plane_count, grid_size, grid_size, field_count),
            "grid",
            split_axis=1,
            concat_axis=0,
            tiled=True,
        )
        field_shape = direct_spectrum.shape
        over_x = jnp.einsum("xvwf,tx->tvwf", direct_spectrum, cas_grid, precision=precise_mode)
        split_view = over_x.reshape(
            field_shape[0], field_shape[1], field_shape[2], atom_count, chain_count
        )
        scaled = split_view * slab_table[..., None]
        back_x = jnp.einsum("tvwar,xt->xvwar", scaled, cas_grid, precision=precise_mode)
        weighted = back_x.reshape(field_shape)
        direct_returned = lax.all_to_all(weighted, "grid", split_axis=0, concat_axis=1, tiled=True)
        fields = direct_returned.reshape(plane_count, grid_size, grid_size, atom_count, chain_count)
        over_z = jnp.einsum("pvwar,zw->pvzar", fields, cas_grid, precision=precise_mode)
        over_y = jnp.einsum("pvzar,yv->arpyz", over_z, cas_grid, precision=precise_mode)
        applied = energies[None, :, None] * lanczos - over_y.reshape(start.shape) / volume
        moments_all = lax.psum(
            (
                moment(lanczos, applied),
                moment(applied, applied),
                moment(lanczos, lanczos),
                moment(previous, previous),
                moment(previous, applied),
                moment(lanczos, previous),
            ),
            ("grid", "band"),
        )
        alpha_now = moments_all[0]
        square = (
            moments_all[1]
            + alpha_now * alpha_now * moments_all[2]
            + beta_prev * beta_prev * moments_all[3]
        )
        square = square - 2.0 * alpha_now * moments_all[0] - 2.0 * beta_prev * moments_all[4]
        square = square + 2.0 * alpha_now * beta_prev * moments_all[5]
        beta_now = jnp.sqrt(square)
        remainder = applied - expand_coef(alpha_now) * lanczos - expand_coef(beta_prev) * previous
        previous = lanczos
        lanczos = remainder / expand_coef(beta_now)
        beta_prev = beta_now
        alpha_list.append(alpha_now)
        beta_list.append(beta_now)
    return (jnp.stack(alpha_list, axis=2), jnp.stack(beta_list, axis=2), lanczos)


def solution(mesh):
    in_specs = (P(None, None, None, "band", "grid"), P(None, "band", "grid"), P(), P())
    out_specs = (P(), P(), P(None, None, None, "band", "grid"))
    return jax.shard_map(body, mesh=mesh, in_specs=in_specs, out_specs=out_specs, check_vma=False)
```

profile of v0, /device:TPU:1, one launch (start us, length us, event | category | flops | bytes accessed | tf_op | source)
XLA Modules:
  0.0 696.7 jit_solution(12863842465715470932)
XLA Ops:
  3.4 41.4 %psum.163 = f32[1,1]{1,0:T(1,128)} all-reduce(f32[1,1]{1,0:T(1,128)} %bitcast.1), channel_id=1, replica_groups=mesh['grid'=8,'band'=4] {'grid','band'}, use_global_device_ids=true, to_apply=%region_1.2 | all-reduce | flops 1 | bytes 8 | tf_op jit(solution)/shard_map/psum | solution.py:54
  46.8 2.7 reshape.300
  49.5 14.6 %fusion.60 = f32[4,32,32,64]{3,2,1,0:T(8,128)S(1)} fusion(f32[64,4,32,32]{3,2,1,0:T(8,128)} %reshape.300), kind=kOutput, calls=%fused_computation.48 | convolution fusion | flops 100678656 | bytes 2097152 | tf_op jit(solution)/shard_map/arpyz,wz->pywar/dot_general | solution.py:62
  64.1 3.0 fusion.40
  70.5 5.3 all-to-all-start
  79.1 8.7 %all-to-all-done = f32[8,1,32768]{2,1,0:T(1,128)S(1)} async-done(((f32[8,1,32768]{2,1,0:T(1,128)}), f32[8,1,32768]{2,1,0:T(1,128)S(1)}, u32[]{:S(2)}, u32[]{:S(2)}) %all-to-all-start) | async-done | bytes 1048608 | tf_op jit(solution)/shard_map/all_to_all | solution.py:68
  88.2 3.1 reduce.21
  92.4 3.0 fusion.28
  100.2 20.3 %all_to_all.132 = f32[8,1,32768]{2,1,0:T(1,128)S(1)} all-to-all(f32[8,1,32768]{2,1,0:T(1,128)S(1)} %reshape.323), channel_id=1, replica_groups=mesh['grid'=8,'band'=4] {'grid'}, dimensions={0} | all-to-all | bytes 2097152 | tf_op jit(solution)/shard_map/all_to_all | solution.py:83
  120.5 3.1 reduce.22
  126.7 3.0 multiply_bitcast_fusion.3
  129.7 4.5 copy.97
  134.2 3.7 div.203
  143.1 43.0 %all-reduce.3 = (f32[1,1]{1,0:T(1,128)}, f32[1,1]{1,0:T(1,128)}, f32[1,1]{1,0:T(1,128)}, f32[1,1]{1,0:T(1,128)}, f32[1,1]{1,0:T(1,128)}, /*index=5*/f32[1,1]{1,0:T(1,128)}) all-reduce(f32[1,1]{1,0:T(1,128)} %bitcast.31, f32[1,1]{1,0:T(1,128)} %bitcast.28, f32[1,1]{1,0:T(1,128)} %bitcast.32, ...), channel_id=1, replica_groups=mesh['grid'=8,'band'=4] {'grid','band'}, use_global_device_ids=true, to_apply=%region_5.6 | all-reduce | flops 6 | bytes 48 | tf_op jit(solution)/shard_map/psum | solution.py:88
  194.1 2.7 reshape.305
  196.8 14.6 %fusion.63 = f32[4,32,32,64]{3,2,1,0:T(8,128)S(1)} fusion(f32[64,4,32,32]{3,2,1,0:T(8,128)} %reshape.305), kind=kOutput, calls=%fused_computation.49 | convolution fusion | flops 100678656 | bytes 2097152 | tf_op jit(solution)/shard_map/arpyz,wz->pywar/dot_general | solution.py:62
  211.4 3.0 fusion.45
  217.0 3.3 reshape.325
  220.4 19.8 %all_to_all.133 = f32[8,1,32768]{2,1,0:T(1,128)} all-to-all(f32[8,1,32768]{2,1,0:T(1,128)} %reshape.325), channel_id=1, replica_groups=mesh['grid'=8,'band'=4] {'grid'}, dimensions={0} | all-to-all | bytes 2097152 | tf_op jit(solution)/shard_map/all_to_all | solution.py:68
  240.2 5.3 reduce.23
  245.5 3.4 reshape.326
  250.7 3.0 fusion.22
  258.5 3.3 reshape.327
  261.8 5.8 all-to-all-start.3
  268.2 11.2 %all-to-all-done.3 = f32[8,1,32768]{2,1,0:T(1,128)} async-done(((f32[8,1,32768]{2,1,0:T(1,128)}), f32[8,1,32768]{2,1,0:T(1,128)}, u32[]{:S(2)}, u32[]{:S(2)}) %all-to-all-start.3) | async-done | bytes 1048608 | tf_op jit(solution)/shard_map/all_to_all | solution.py:83
  279.5 5.3 reduce.24
  284.8 3.4 reshape.328
  292.0 4.4 multiply_bitcast_fusion.2
  296.3 5.6 copy.107
  301.9 4.3 div.220
  306.2 3.3 multiply_reduce_fusion.10
  312.7 43.9 %all-reduce.2 = (f32[1,1]{1,0:T(1,128)}, f32[1,1]{1,0:T(1,128)}, f32[1,1]{1,0:T(1,128)}, f32[1,1]{1,0:T(1,128)}, f32[1,1]{1,0:T(1,128)}) all-reduce(f32[1,1]{1,0:T(1,128)} %bitcast.57, f32[1,1]{1,0:T(1,128)} %bitcast.54, f32[1,1]{1,0:T(1,128)} %bitcast.58, f32[1,1]{1,0:T(1,128)} %bitcast.59, ...), channel_id=1, replica_groups=mesh['grid'=8,'band'=4] {'grid','band'}, use_global_device_ids=true, to_apply=%region_16.17 | all-reduce | flops 5 | bytes 40 | tf_op jit(solution)/shard_map/psum | solution.py:88
  363.6 2.7 reshape.310
  366.3 14.6 %fusion.66 = f32[4,32,32,64]{3,2,1,0:T(8,128)S(1)} fusion(f32[64,4,32,32]{3,2,1,0:T(8,128)} %reshape.310), kind=kOutput, calls=%fused_computation.50 | convolution fusion | flops 100678656 | bytes 2097152 | tf_op jit(solution)/shard_map/arpyz,wz->pywar/dot_general | solution.py:62
  381.0 3.0 fusion.50
  389.1 19.2 %all_to_all.134 = f32[8,1,32768]{2,1,0:T(1,128)} all-to-all(f32[8,1,32768]{2,1,0:T(1,128)S(1)} %reshape.329), channel_id=1, replica_groups=mesh['grid'=8,'band'=4] {'grid'}, dimensions={0} | all-to-all | bytes 2097152 | tf_op jit(solution)/shard_map/all_to_all | solution.py:68
  408.4 4.4 reduce.25
  416.7 3.0 fusion.16
  424.5 3.3 reshape.331
  427.8 5.8 all-to-all-start.5
  434.2 11.2 %all-to-all-done.5 = f32[8,1,32768]{2,1,0:T(1,128)} async-done(((f32[8,1,32768]{2,1,0:T(1,128)}), f32[8,1,32768]{2,1,0:T(1,128)}, u32[]{:S(2)}, u32[]{:S(2)}) %all-to-all-start.5) | async-done | bytes 1048608 | tf_op jit(solution)/shard_map/all_to_all | solution.py:83
  445.5 4.4 reduce.26
  455.8 4.4 multiply_bitcast_fusion.1
  460.1 5.6 copy.117
  465.8 4.4 div.237
  470.2 3.3 multiply_reduce_fusion.5
  476.6 44.8 %all-reduce.1 = (f32[1,1]{1,0:T(1,128)}, f32[1,1]{1,0:T(1,128)}, f32[1,1]{1,0:T(1,128)}, f32[1,1]{1,0:T(1,128)}, f32[1,1]{1,0:T(1,128)}) all-reduce(f32[1,1]{1,0:T(1,128)} %bitcast.83, f32[1,1]{1,0:T(1,128)} %bitcast.80, f32[1,1]{1,0:T(1,128)} %bitcast.84, f32[1,1]{1,0:T(1,128)} %bitcast.85, ...), channel_id=1, replica_groups=mesh['grid'=8,'band'=4] {'grid','band'}, use_global_device_ids=true, to_apply=%region_26.27 | all-reduce | flops 5 | bytes 40 | tf_op jit(solution)/shard_map/psum | solution.py:88
  528.2 2.7 reshape.315
  530.9 14.6 %fusion.69 = f32[4,32,32,64]{3,2,1,0:T(8,128)S(1)} fusion(f32[64,4,32,32]{3,2,1,0:T(8,128)} %reshape.315), kind=kOutput, calls=%fused_computation.51 | convolution fusion | flops 100678656 | bytes 2097152 | tf_op jit(solution)/shard_map/arpyz,wz->pywar/dot_general | solution.py:62
  545.5 3.0 fusion.55
  553.7 19.3 %all_to_all.135 = f32[8,1,32768]{2,1,0:T(1,128)} all-to-all(f32[8,1,32768]{2,1,0:T(1,128)S(1)} %reshape.333), channel_id=1, replica_groups=mesh['grid'=8,'band'=4] {'grid'}, dimensions={0} | all-to-all | bytes 2097152 | tf_op jit(solution)/shard_map/all_to_all | solution.py:68
  573.0 4.4 reduce.27
  581.4 3.0 fusion.10
  589.1 3.3 reshape.335
  592.5 5.7 all-to-all-start.7
  598.8 11.2 %all-to-all-done.7 = f32[8,1,32768]{2,1,0:T(1,128)} async-done(((f32[8,1,32768]{2,1,0:T(1,128)}), f32[8,1,32768]{2,1,0:T(1,128)}, u32[]{:S(2)}, u32[]{:S(2)}) %all-to-all-start.7) | async-done | bytes 1048608 | tf_op jit(solution)/shard_map/all_to_all | solution.py:83
  610.0 4.4 reduce.28
  620.3 4.4 multiply_bitcast_fusion
  624.6 5.6 copy.127
  630.3 4.4 div.254
  634.7 3.3 multiply_reduce_fusion
  641.2 43.6 %all-reduce = (f32[1,1]{1,0:T(1,128)}, f32[1,1]{1,0:T(1,128)}, f32[1,1]{1,0:T(1,128)}, f32[1,1]{1,0:T(1,128)}, f32[1,1]{1,0:T(1,128)}) all-reduce(f32[1,1]{1,0:T(1,128)} %bitcast.106, f32[1,1]{1,0:T(1,128)} %bitcast.111, f32[1,1]{1,0:T(1,128)} %bitcast.112, ...), channel_id=1, replica_groups=mesh['grid'=8,'band'=4] {'grid','band'}, use_global_device_ids=true, to_apply=%region_34.35 | all-reduce | flops 5 | bytes 40 | tf_op jit(solution)/shard_map/psum | solution.py:88
  690.1 3.1 divide_bitcast_fusion
  693.2 3.0 pad_maximum_fusion
  (58 shorter events, 77.6 us)
Async XLA Ops:
  68.3 7.4 %copy-start.5 = (s32[3,1]{0,1:T(1,128)S(1)}, s32[3,1]{0,1:T(1,128)}, u32[]{:S(2)}) copy-start(s32[3,1]{0,1:T(1,128)} %param.6) | copy-start | bytes 40
  68.4 10.1 %copy-start.4 = (f32[32,32,32]{2,1,0:T(8,128)S(1)}, f32[32,32,32]{2,1,0:T(8,128)}, u32[]{:S(2)}) copy-start(f32[32,32,32]{2,1,0:T(8,128)} %param.7) | copy-start | bytes 393220
  70.5 17.2 %all-to-all-start = ((f32[8,1,32768]{2,1,0:T(1,128)}), f32[8,1,32768]{2,1,0:T(1,128)S(1)}, u32[]{:S(2)}, u32[]{:S(2)}) async-start(f32[8,1,32768]{2,1,0:T(1,128)} %reshape.321), calls=%async_computation | async-start | bytes 2097152 | tf_op jit(solution)/shard_map/all_to_all | solution.py:68
  134.2 3.7 copy-start
  134.2 3.7 copy-start.1
  261.8 17.7 %all-to-all-start.3 = ((f32[8,1,32768]{2,1,0:T(1,128)}), f32[8,1,32768]{2,1,0:T(1,128)}, u32[]{:S(2)}, u32[]{:S(2)}) async-start(f32[8,1,32768]{2,1,0:T(1,128)} %reshape.327), calls=%async_computation.3 | async-start | bytes 2097152 | tf_op jit(solution)/shard_map/all_to_all | solution.py:83
  427.8 17.7 %all-to-all-start.5 = ((f32[8,1,32768]{2,1,0:T(1,128)}), f32[8,1,32768]{2,1,0:T(1,128)}, u32[]{:S(2)}, u32[]{:S(2)}) async-start(f32[8,1,32768]{2,1,0:T(1,128)} %reshape.331), calls=%async_computation.5 | async-start | bytes 2097152 | tf_op jit(solution)/shard_map/all_to_all | solution.py:83
  465.8 4.4 copy-start.2
  592.5 17.5 %all-to-all-start.7 = ((f32[8,1,32768]{2,1,0:T(1,128)}), f32[8,1,32768]{2,1,0:T(1,128)}, u32[]{:S(2)}, u32[]{:S(2)}) async-start(f32[8,1,32768]{2,1,0:T(1,128)} %reshape.335), calls=%async_computation.7 | async-start | bytes 2097152 | tf_op jit(solution)/shard_map/all_to_all | solution.py:83
  630.3 4.4 copy-start.3
where the time goes:
time: 709 us; the launch traced here: 697 us
  blocking collectives  295 us (42%)
  local copies, waits for them, and re-layouts  118 us (17%)
  matrix products  115 us (16%)
  other arithmetic  62.4 us (9%)
  waiting for transfers between devices  42.4 us (6%)
  between operations  40.5 us (6%)
  starting transfers between devices  22.6 us (3%)
    psum x4, blocking collectives, body(): lax.psum((moment(lanczos, applied), moment(applied, applied), moment(lanc...  175 us
    dot_general x4, matrix products, body(): jnp.einsum('arpyz,wz->pywar', spread_fields, cas_grid, precision=precise_...  58.4 us
    all_to_all x3, blocking collectives, body(): lax.all_to_all(spread_over_y.reshape(plane_count, grid_size, grid_size, f...  58.4 us
    psum x1, blocking collectives, body(): start_sum = lax.psum(moment(start, start), ('grid', 'band'))  41.4 us
    unnamed x28, local copies, waits for them, and re-layouts  39.2 us
    div x8, local copies, waits for them, and re-layouts, body(): over_y.reshape(start.shape) / volume  38.1 us
    all_to_all x3, waiting for transfers between devices, body(): lax.all_to_all(weighted, 'grid', split_axis=0, concat_axis=1, tiled=True)  33.7 us
    all_to_all x1, blocking collectives, body(): lax.all_to_all(weighted, 'grid', split_axis=0, concat_axis=1, tiled=True)  20.3 us
  transfers between devices with their start and end apart: 4, of which 4 were waited for; matrix products, arithmetic and copies ran while one was open for 0% of the time, Pallas kernels for 0%

commit v1 on v0

--- a/solution.py
+++ b/solution.py
@@ -1,8 +1,12 @@
+import functools
 import math
 
 import jax
 import jax.numpy as jnp
+import numpy as np
 from jax import lax
+from jax.experimental import pallas as pl
+from jax.experimental.pallas import tpu as pltpu
 from jax.sharding import PartitionSpec as P
 
 ITERS = 4
@@ -29,7 +33,7 @@
     return values[:, None, :, None, None]
 
 
-def body(start, energies, sites, potential):
+def plane_body(start, energies, sites, potential):
     grid_size = potential.shape[0]
     volume = grid_size * grid_size * grid_size
     atom_count, core_count, pol_count, band_local, kpoint_local = start.shape
@@ -114,6 +118,254 @@
     return (jnp.stack(alpha_list, axis=2), jnp.stack(beta_list, axis=2), lanczos)
 
 
+MESH = pl.DeviceIdType.MESH
+LANES = 128
+SUBLANES = 8
+
+
+def split(value):
+    high = value.astype(jnp.bfloat16)
+    return high, (value - high.astype(jnp.float32)).astype(jnp.bfloat16)
+
+
+def dot3(left, right):
+    left_high, left_low = left
+    right_high, right_low = right
+    total = jnp.dot(left_high, right_high, preferred_element_type=jnp.float32)
+    total += jnp.dot(left_low, right_high, preferred_element_type=jnp.float32)
+    return total + jnp.dot(left_high, right_low, preferred_element_type=jnp.float32)
+
+
+def shifted_potential(table, sites, grid_size):
+    cells = grid_size * grid_size
+    lane = lax.broadcasted_iota(jnp.int32, table.shape, 1) % grid_size
+    for axis in range(3):
+        step = 1
+        while step < grid_size:
+            if axis == 0:
+                moved = pltpu.roll(table, step, 0)
+            elif axis == 1:
+                moved = pltpu.roll(table, step * grid_size, 1)
+            else:
+                moved = jnp.where(
+                    lane >= step,
+                    pltpu.roll(table, step, 1),
+                    pltpu.roll(table, cells - grid_size + step, 1),
+                )
+            flag = jnp.full(table.shape, sites[axis, 0] // step % 2, jnp.int32)
+            table = jnp.where(flag == 1, moved, table)
+            step *= 2
+    return table
+
+
+def recursion_kernel(
+    sizes, start, energies, sites, pot, y_table, z_table, x_high, x_low,
+    out, coef,
+    got, got_energies, vec, prev, applied, energy, site_table, vec_high, vec_low,
+    mid_high, mid_low, mat_high, mat_low, outgoing, grid_sums, band_sums,
+    start_send, start_recv, energy_send, energy_recv, out_send, out_recv,
+    grid_send, grid_recv, band_send, band_recv,
+):
+    n, band_n, grid_size, halves, block = sizes
+    me = lax.axis_index("grid")
+    band_me = lax.axis_index("band")
+    cells = grid_size * grid_size
+    planes = grid_size // n
+    rows = grid_size * SUBLANES
+    total_count = float(rows * cells * n * band_n)
+
+    barrier = pltpu.get_barrier_semaphore()
+    for k in range(1, n):
+        pl.semaphore_signal(barrier, inc=1, device_id={"grid": (me + k) % n}, device_id_type=MESH)
+    for k in range(1, band_n):
+        pl.semaphore_signal(barrier, inc=1, device_id={"band": (band_me + k) % band_n}, device_id_type=MESH)
+    pl.semaphore_wait(barrier, n + band_n - 2)
+
+    def start_piece(owner):
+        return start.at[0, owner // halves, 0, pl.ds(pl.multiple_of(owner % halves * SUBLANES, SUBLANES), SUBLANES), :]
+
+    def energy_piece(owner):
+        return energies.at[owner // halves, pl.ds(pl.multiple_of(owner % halves * SUBLANES, SUBLANES), SUBLANES), :]
+
+    def out_piece(owner):
+        return out.at[0, owner // halves, 0, pl.ds(pl.multiple_of(owner % halves * SUBLANES, SUBLANES), SUBLANES), :]
+
+    def spread(piece, landing, send, recv):
+        copies = []
+        for k in range(1, n):
+            peer = (me + k) % n
+            copies.append(pltpu.make_async_remote_copy(
+                src_ref=piece(peer), dst_ref=landing.at[me], send_sem=send.at[k], recv_sem=recv.at[k],
+                device_id={"grid": peer}, device_id_type=MESH))
+        own = pltpu.make_async_copy(piece(me), landing.at[me], send.at[0])
+        for copy in copies:
+            copy.start()
+        own.start()
+        return copies + [own]
+
+    start_copies = spread(start_piece, got, start_send, start_recv)
+    energy_copies = spread(energy_piece, got_energies, energy_send, energy_recv)
+
+    def matrix_rows(y, carry):
+        high, low = split(y_table[pl.ds(y, 1), :] * z_table[...])
+        at = pl.ds(pl.multiple_of(y * grid_size, grid_size), grid_size)
+        mat_high[at, :] = high
+        mat_low[at, :] = low
+        return carry
+
+    lax.fori_loop(0, grid_size, matrix_rows, 0)
+    table = shifted_potential(pot[...], sites, grid_size) * (1.0 / (grid_size * cells))
+    for x in range(grid_size):
+        site_table[SUBLANES * x:SUBLANES * (x + 1), :] = jnp.broadcast_to(table[x:x + 1, :], (SUBLANES, cells))
+    prev[...] = jnp.zeros_like(prev)
+
+    for copy in start_copies:
+        copy.wait()
+    for x in range(grid_size):
+        at = slice(SUBLANES * x, SUBLANES * (x + 1))
+        vec[at, :] = got[x // planes, :, x % planes * cells:(x % planes + 1) * cells]
+    vec_high[...], vec_low[...] = split(vec[...])
+
+    blocks = [slice(i, i + block) for i in range(0, cells, block)]
+    lane = lax.broadcasted_iota(jnp.int32, (1, LANES), 1)
+
+    def step(j, carry):
+        alphas, betas, beta_prev = carry
+        x_pair = (x_high[...], x_low[...])
+        for cols in blocks:
+            mat = (mat_high[:, cols], mat_low[:, cols])
+            spectrum = dot3((vec_high[...], vec_low[...]), mat)
+            spectrum = dot3(x_pair, split(spectrum)) * site_table[:, cols]
+            mid_high[:, cols], mid_low[:, cols] = split(dot3(x_pair, split(spectrum)))
+
+        @pl.when(j == 0)
+        def _():
+            for copy in energy_copies:
+                copy.wait()
+            for x in range(grid_size):
+                at = slice(SUBLANES * x, SUBLANES * (x + 1))
+                energy[at, :] = got_energies[x // planes, :, x % planes * cells:(x % planes + 1) * cells]
+
+        sums = [jnp.zeros((1, block), jnp.float32)] * 6
+        for cols in blocks:
+            mat = (mat_high[:, cols], mat_low[:, cols])
+            here, before = vec[:, cols], prev[:, cols]
+            new = energy[:, cols] * here - dot3((mid_high[...], mid_low[...]), mat)
+            applied[:, cols] = new
+            for i, (a, b) in enumerate(((here, new), (new, new), (here, here), (before, before), (before, new), (here, before))):
+                sums[i] = sums[i] + jnp.sum(a * b, axis=0, keepdims=True)
+        message = jnp.zeros((1, LANES), jnp.float32)
+        for i in range(6):
+            message = jnp.where(lane == i, jnp.sum(sums[i], axis=1, keepdims=True), message)
+
+        def total(message, buffer, axis, size, my, send, recv):
+            buffer[j, my] = message
+            copies = []
+            for k in range(1, size):
+                copy = pltpu.make_async_remote_copy(
+                    src_ref=buffer.at[j, my], dst_ref=buffer.at[j, my], send_sem=send.at[j, k], recv_sem=recv.at[j, k],
+                    device_id={axis: (my + k) % size}, device_id_type=MESH)
+                copy.start()
+                copies.append(copy)
+            for copy in copies:
+                copy.wait()
+            return jnp.sum(buffer[j], axis=0)
+
+        message = total(message, grid_sums, "grid", n, me, grid_send, grid_recv)
+        message = total(message, band_sums, "band", band_n, band_me, band_send, band_recv)
+        m = [jnp.sum(jnp.where(lane == i, message, 0.0), axis=1, keepdims=True) / total_count for i in range(6)]
+        norm = jnp.where(jnp.full((1, 1), j, jnp.int32) == 0, m[2], 1.0)
+        scale = jnp.sqrt(norm)
+        alpha = m[0] / norm
+        square = m[1] / norm + alpha * alpha * (m[2] / norm) + beta_prev * beta_prev * m[3]
+        square = square - 2.0 * alpha * alpha - 2.0 * beta_prev * m[4]
+        square = square + 2.0 * alpha * beta_prev * m[5]
+        beta = jnp.sqrt(square)
+        to_new = 1.0 / (scale * beta)
+        to_here = alpha * to_new
+        to_before = beta_prev / beta
+        to_prev = 1.0 / scale
+        for x in range(0, grid_size, planes):
+            at = slice(SUBLANES * x, SUBLANES * (x + planes))
+            here = vec[at, :]
+            value = to_new * applied[at, :] - to_here * here - to_before * prev[at, :]
+            prev[at, :] = to_prev * here
+            vec[at, :] = value
+            vec_high[at, :], vec_low[at, :] = split(value)
+        alphas = jnp.where(lane == j, alpha, alphas)
+        betas = jnp.where(lane == j, beta, betas)
+        return alphas, betas, beta
+
+    zeros = jnp.zeros((1, LANES), jnp.float32)
+    alphas, betas, _ = lax.fori_loop(0, ITERS, step, (zeros, zeros, jnp.zeros((1, 1), jnp.float32)))
+    coef[0:1, :] = alphas
+    coef[1:2, :] = betas
+    for x in range(grid_size):
+        at = slice(SUBLANES * x, SUBLANES * (x + 1))
+        outgoing[x // planes, :, x % planes * cells:(x % planes + 1) * cells] = vec[at, :]
+    out_copies = []
+    for k in range(1, n):
+        peer = (me + k) % n
+        out_copies.append(pltpu.make_async_remote_copy(
+            src_ref=outgoing.at[peer], dst_ref=out_piece(me), send_sem=out_send.at[k], recv_sem=out_recv.at[k],
+            device_id={"grid": peer}, device_id_type=MESH))
+    out_copies.append(pltpu.make_async_copy(outgoing.at[me], out_piece(me), out_send.at[0]))
+    for copy in out_copies:
+        copy.start()
+    for copy in out_copies:
+        copy.wait()
+
+
+def field_body(start, energies, sites, potential):
+    grid_size = potential.shape[0]
+    cells = grid_size * grid_size
+    n, band_n = lax.axis_size("grid"), lax.axis_size("band")
+    halves = start.shape[3] // SUBLANES
+    rows = grid_size * SUBLANES
+    index = np.arange(grid_size)
+    angle = (index[:, None] * index[None, :] % grid_size) * (2.0 * math.pi / grid_size)
+    cas = np.cos(angle) + np.sin(angle)
+    y_table = jnp.asarray(np.repeat(cas, grid_size, axis=1), jnp.float32)
+    z_table = jnp.asarray(np.tile(cas, (1, grid_size)), jnp.float32)
+    x_wide = np.kron(cas, np.eye(SUBLANES)).astype(np.float32)
+    x_high = x_wide.astype(jnp.bfloat16)
+    x_low = (x_wide - x_high.astype(np.float32)).astype(jnp.bfloat16)
+    vmem = pl.BlockSpec(memory_space=pltpu.VMEM)
+    hbm = pl.BlockSpec(memory_space=pl.ANY)
+    slab = (n, SUBLANES, start.shape[4])
+    full = pltpu.VMEM((rows, cells), jnp.float32)
+    half = pltpu.VMEM((rows, cells), jnp.bfloat16)
+    dma = pltpu.SemaphoreType.DMA
+    out, coef = pl.pallas_call(
+        functools.partial(recursion_kernel, (n, band_n, grid_size, halves, min(256, cells))),
+        out_shape=(jax.ShapeDtypeStruct(start.shape, jnp.float32), jax.ShapeDtypeStruct((2, LANES), jnp.float32)),
+        in_specs=[hbm, hbm, pl.BlockSpec(memory_space=pltpu.SMEM)] + [vmem] * 5,
+        out_specs=(hbm, vmem),
+        scratch_shapes=[
+            pltpu.VMEM(slab, jnp.float32), pltpu.VMEM(slab, jnp.float32),
+            full, full, full, full, full, half, half, half, half,
+            pltpu.VMEM((cells, cells), jnp.bfloat16), pltpu.VMEM((cells, cells), jnp.bfloat16),
+            pltpu.VMEM(slab, jnp.float32),
+            pltpu.VMEM((ITERS, n, 1, LANES), jnp.float32), pltpu.VMEM((ITERS, band_n, 1, LANES), jnp.float32),
+            dma((n,)), dma((n,)), dma((n,)), dma((n,)), dma((n,)), dma((n,)),
+            dma((ITERS, n)), dma((ITERS, n)), dma((ITERS, band_n)), dma((ITERS, band_n)),
+        ],
+        compiler_params=pltpu.CompilerParams(collective_id=0, has_side_effects=True, vmem_limit_bytes=50 * 1024 * 1024),
+    )(start, energies, sites, potential.reshape(grid_size, cells), y_table, z_table, jnp.asarray(x_high), jnp.asarray(x_low))
+    return coef[0, :ITERS].reshape(1, 1, ITERS), coef[1, :ITERS].reshape(1, 1, ITERS), out
+
+
+def body(start, energies, sites, potential):
+    atoms, cores, pols, bands, _ = start.shape
+    grid_size = potential.shape[0]
+    whole_fields = (
+        atoms == 1 and pols == 1 and bands % SUBLANES == 0
+        and cores * bands == SUBLANES * lax.axis_size("grid")
+        and grid_size % SUBLANES == 0 and grid_size * grid_size % LANES == 0
+    )
+    return (field_body if whole_fields else plane_body)(start, energies, sites, potential)
+
+
 def solution(mesh):
     in_specs = (P(None, None, None, "band", "grid"), P(None, "band", "grid"), P(), P())
     out_specs = (P(), P(), P(None, None, None, "band", "grid"))

time: 709 us -> 104 us (0.15); the launches traced: 697 us -> 104 us
  blocking collectives: 295 us -> 0 us
  matrix products: 115 us -> 0 us
  local copies, waits for them, and re-layouts: 118 us -> 6.02 us
  Pallas kernels: 0 us -> 97.3 us
  other arithmetic: 62.4 us -> 0 us
  waiting for transfers between devices: 42.4 us -> 0 us
  between operations: 40.5 us -> 0.69 us
  starting transfers between devices: 22.6 us -> 0 us
    psum x5 -> x0, blocking collectives: 217 us -> none  [the longest x4 175 us: body(): lax.psum((moment(lanczos, applied), moment(applied, applied), moment(lanc...]
    dot_general x24 -> x0, matrix products: 115 us -> none  [the longest x4 58.4 us: body(): jnp.einsum('arpyz,wz->pywar', spread_fields, cas_grid, precision=precise_...]
    pallas_call x0 -> x1, Pallas kernels: none -> 97.3 us  [field_body(): pl.pallas_call(functools.partial(recursion_kernel, (n, band_n, grid_size,...]
    all_to_all x4 -> x0, blocking collectives: 78.7 us -> none  [the longest x3 58.4 us: body(): lax.all_to_all(spread_over_y.reshape(plane_count, grid_size, grid_size, f...]
    all_to_all x4 -> x0, waiting for transfers between devices: 42.4 us -> none  [the longest x3 33.7 us: body(): lax.all_to_all(weighted, 'grid', split_axis=0, concat_axis=1, tiled=True)]
    div x8 -> x0, local copies, waits for them, and re-layouts: 38.1 us -> none  [body(): over_y.reshape(start.shape) / volume]
    unnamed x28 -> x14, local copies, waits for them, and re-layouts: 39.2 us -> 4.17 us
    all_to_all x8 -> x0, other arithmetic: 34.4 us -> none  [the longest x4 17.2 us: body(): lax.all_to_all(spread_over_y.reshape(plane_count, grid_size, grid_size, f...]
  transfers between devices with their start and end apart: 4 -> 0, of which waited for: 4 -> 0; matrix products, arithmetic and copies ran while one was open for 0% -> 0% of each run, Pallas kernels for 0% -> 0%
where the time goes in v1:
time: 104 us
  Pallas kernels  97.3 us (94%)
  local copies, waits for them, and re-layouts  6.02 us (6%)
    pallas_call x1, Pallas kernels, field_body(): pl.pallas_call(functools.partial(recursion_kernel, (n, band_n, grid_size,...  97.3 us
    unnamed x14, local copies, waits for them, and re-layouts  4.17 us

profile of v1, /device:TPU:1, one launch (start us, length us, event | category | flops | bytes accessed | tf_op | source)
XLA Modules:
  0.0 104.0 jit_solution(285551369308779305)
XLA Ops:
  0.6 0.7 copy.11.sites
  1.4 0.0 copy-start.2
  1.4 0.0 copy-start.3
  1.4 0.0 copy-start.4
  1.4 0.0 copy-start.5
  1.4 1.3 %reshape.9.pot = f32[32,1024]{1,0:T(8,128)S(1)} reshape(f32[32,32,32]{2,1,0:T(8,128)} %param.11) | data formatting | bytes 262144 | tf_op jit(solution)/shard_map/reshape | solution.py:354
  2.7 0.0 copy-done.2
  2.7 0.0 copy-done.3
  2.7 0.0 copy-done.4
  2.8 0.0 copy-done.5
  2.8 0.0 copy-start
  2.8 1.2 %copy-done = f32[1,4,1,16,4096]{4,3,2,1,0:T(8,128)S(1)} copy-done((f32[1,4,1,16,4096]{4,3,2,1,0:T(8,128)S(1)}, f32[1,4,1,16,4096]{4,3,2,1,0:T(8,128)}, u32[]{:S(2)}) %copy-start) | copy-done | bytes 1048600
  4.0 0.0 copy-start.1
  4.0 1.2 %copy-done.1 = f32[4,16,4096]{2,1,0:T(8,128)S(1)} copy-done((f32[4,16,4096]{2,1,0:T(8,128)S(1)}, f32[4,16,4096]{2,1,0:T(8,128)}, u32[]{:S(2)}) %copy-start.1) | copy-done | bytes 1048600
  5.2 97.3 %shard_map.103 = (f32[1,4,1,16,4096]{4,3,2,1,0:T(8,128)S(1)}, f32[2,128]{1,0:T(2,128)S(1)}) custom-call(f32[1,4,1,16,4096]{4,3,2,1,0:T(8,128)S(1)} %copy-done, f32[4,16,4096]{2,1,0:T(8,128)S(1)} %copy-done.1, s32[3,1]{1,0:T(4,128)S(1)} %copy.11.sites, f32[32,1024]{1,0:T(8,128)S(1)} %reshape.9.pot, f32[32,1024]{1,0:T(8,128)S(1)} %copy-done.5, ...), custom_call_target="tpu_custom_call" | custom-call | tf_op jit(solution)/shard_map/pallas_call | solution.py:339
  102.6 0.5 slice_bitcast_fusion
  103.1 1.0 copy.13
Async XLA Ops:
  1.4 1.4 %copy-start.2 = (bf16[256,256]{1,0:T(8,128)(2,1)S(1)}, bf16[256,256]{1,0:T(8,128)(2,1)}, u32[]{:S(2)}) copy-start(bf16[256,256]{1,0:T(8,128)(2,1)} %constant.11.clone.x_low) | copy-start | bytes 393220
  1.4 1.4 %copy-start.3 = (bf16[256,256]{1,0:T(8,128)(2,1)S(1)}, bf16[256,256]{1,0:T(8,128)(2,1)}, u32[]{:S(2)}) copy-start(bf16[256,256]{1,0:T(8,128)(2,1)} %constant.10.clone.x_high) | copy-start | bytes 393220
  1.4 1.4 %copy-start.4 = (f32[32,1024]{1,0:T(8,128)S(1)}, f32[32,1024]{1,0:T(8,128)}, u32[]{:S(2)}) copy-start(f32[32,1024]{1,0:T(8,128)} %constant.9.clone.z_table) | copy-start | bytes 393220
  1.4 1.4 %copy-start.5 = (f32[32,1024]{1,0:T(8,128)S(1)}, f32[32,1024]{1,0:T(8,128)}, u32[]{:S(2)}) copy-start(f32[32,1024]{1,0:T(8,128)} %constant.8.clone.y_table) | copy-start | bytes 393220
  2.8 1.2 %copy-start = (f32[1,4,1,16,4096]{4,3,2,1,0:T(8,128)S(1)}, f32[1,4,1,16,4096]{4,3,2,1,0:T(8,128)}, u32[]{:S(2)}) copy-start(f32[1,4,1,16,4096]{4,3,2,1,0:T(8,128)} %start.1) | copy-start | bytes 3145732
  4.0 1.2 %copy-start.1 = (f32[4,16,4096]{2,1,0:T(8,128)S(1)}, f32[4,16,4096]{2,1,0:T(8,128)}, u32[]{:S(2)}) copy-start(f32[4,16,4096]{2,1,0:T(8,128)} %energies.1) | copy-start | bytes 3145732

commit v2 on v1

--- a/solution.py
+++ b/solution.py
@@ -152,7 +152,7 @@
                     pltpu.roll(table, step, 1),
                     pltpu.roll(table, cells - grid_size + step, 1),
                 )
-            flag = jnp.full(table.shape, sites[axis, 0] // step % 2, jnp.int32)
+            flag = jnp.full(table.shape, sites[axis] // step % 2, jnp.int32)
             table = jnp.where(flag == 1, moved, table)
             step *= 2
     return table
@@ -160,10 +160,10 @@
 
 def recursion_kernel(
     sizes, start, energies, sites, pot, y_table, z_table, x_high, x_low,
-    out, coef,
-    got, got_energies, vec, prev, applied, energy, site_table, vec_high, vec_low,
+    out, alphas_out, betas_out,
+    pot_here, pot_flat, got, got_energies, vec, prev, applied, applied_prev, twice, energy, site_table, vec_high, vec_low,
     mid_high, mid_low, mat_high, mat_low, outgoing, grid_sums, band_sums,
-    start_send, start_recv, energy_send, energy_recv, out_send, out_recv,
+    pot_sem, start_send, start_recv, energy_send, energy_recv, out_send, out_recv,
     grid_send, grid_recv, band_send, band_recv,
 ):
     n, band_n, grid_size, halves, block = sizes
@@ -174,6 +174,8 @@
     rows = grid_size * SUBLANES
     total_count = float(rows * cells * n * band_n)
 
+    pot_copy = pltpu.make_async_copy(pot, pot_here, pot_sem)
+    pot_copy.start()
     barrier = pltpu.get_barrier_semaphore()
     for k in range(1, n):
         pl.semaphore_signal(barrier, inc=1, device_id={"grid": (me + k) % n}, device_id_type=MESH)
@@ -214,10 +216,14 @@
         return carry
 
     lax.fori_loop(0, grid_size, matrix_rows, 0)
-    table = shifted_potential(pot[...], sites, grid_size) * (1.0 / (grid_size * cells))
+    pot_copy.wait()
+    for y in range(grid_size):
+        pot_flat[:, y * grid_size:(y + 1) * grid_size] = pot_here[:, y, :]
+    table = shifted_potential(pot_flat[...], sites, grid_size) * (1.0 / (grid_size * cells))
     for x in range(grid_size):
         site_table[SUBLANES * x:SUBLANES * (x + 1), :] = jnp.broadcast_to(table[x:x + 1, :], (SUBLANES, cells))
     prev[...] = jnp.zeros_like(prev)
+    applied_prev[...] = jnp.zeros_like(prev)
 
     for copy in start_copies:
         copy.wait()
@@ -228,9 +234,10 @@
 
     blocks = [slice(i, i + block) for i in range(0, cells, block)]
     lane = lax.broadcasted_iota(jnp.int32, (1, LANES), 1)
-
-    def step(j, carry):
-        alphas, betas, beta_prev = carry
+    tall = 2 * SUBLANES
+    zero_sums = (jnp.zeros((SUBLANES, block), jnp.float32),) * 6
+
+    def to_site_and_back():
         x_pair = (x_high[...], x_low[...])
         for cols in blocks:
             mat = (mat_high[:, cols], mat_low[:, cols])
@@ -238,41 +245,50 @@
             spectrum = dot3(x_pair, split(spectrum)) * site_table[:, cols]
             mid_high[:, cols], mid_low[:, cols] = split(dot3(x_pair, split(spectrum)))
 
-        @pl.when(j == 0)
-        def _():
-            for copy in energy_copies:
-                copy.wait()
-            for x in range(grid_size):
-                at = slice(SUBLANES * x, SUBLANES * (x + 1))
-                energy[at, :] = got_energies[x // planes, :, x % planes * cells:(x % planes + 1) * cells]
-
-        sums = [jnp.zeros((1, block), jnp.float32)] * 6
+    def finish_apply(source, target):
         for cols in blocks:
             mat = (mat_high[:, cols], mat_low[:, cols])
-            here, before = vec[:, cols], prev[:, cols]
-            new = energy[:, cols] * here - dot3((mid_high[...], mid_low[...]), mat)
-            applied[:, cols] = new
-            for i, (a, b) in enumerate(((here, new), (new, new), (here, here), (before, before), (before, new), (here, before))):
-                sums[i] = sums[i] + jnp.sum(a * b, axis=0, keepdims=True)
+            target[:, cols] = energy[:, cols] * source[:, cols] - dot3((mid_high[...], mid_low[...]), mat)
+
+    def folded(a, b):
+        product = a * b
+        return product[:SUBLANES] + product[SUBLANES:]
+
+    def add_moments(sums, here, new, before):
+        pairs = ((here, new), (new, new), (here, here), (before, before), (before, new), (here, before))
+        return tuple(total + folded(a, b) for total, (a, b) in zip(sums, pairs))
+
+    def message_of(sums):
         message = jnp.zeros((1, LANES), jnp.float32)
         for i in range(6):
-            message = jnp.where(lane == i, jnp.sum(sums[i], axis=1, keepdims=True), message)
-
-        def total(message, buffer, axis, size, my, send, recv):
-            buffer[j, my] = message
-            copies = []
-            for k in range(1, size):
-                copy = pltpu.make_async_remote_copy(
-                    src_ref=buffer.at[j, my], dst_ref=buffer.at[j, my], send_sem=send.at[j, k], recv_sem=recv.at[j, k],
-                    device_id={axis: (my + k) % size}, device_id_type=MESH)
-                copy.start()
-                copies.append(copy)
+            value = jnp.sum(jnp.sum(sums[i], axis=0, keepdims=True), axis=1, keepdims=True)
+            message = jnp.where(lane == i, value, message)
+        return message
+
+    def exchange(j, message, buffer, axis, size, my, send, recv):
+        buffer[j, my] = message
+        copies = []
+        for k in range(1, size):
+            copy = pltpu.make_async_remote_copy(
+                src_ref=buffer.at[j, my], dst_ref=buffer.at[j, my], send_sem=send.at[j, k], recv_sem=recv.at[j, k],
+                device_id={axis: (my + k) % size}, device_id_type=MESH)
+            copy.start()
+            copies.append(copy)
+
+        def total():
             for copy in copies:
                 copy.wait()
             return jnp.sum(buffer[j], axis=0)
 
-        message = total(message, grid_sums, "grid", n, me, grid_send, grid_recv)
-        message = total(message, band_sums, "band", band_n, band_me, band_send, band_recv)
+        return total
+
+    def over_grid(j, message):
+        return exchange(j, message, grid_sums, "grid", n, me, grid_send, grid_recv)
+
+    def over_band(j, message):
+        return exchange(j, message, band_sums, "band", band_n, band_me, band_send, band_recv)
+
+    def coefficients(j, message, beta_prev):
         m = [jnp.sum(jnp.where(lane == i, message, 0.0), axis=1, keepdims=True) / total_count for i in range(6)]
         norm = jnp.where(jnp.full((1, 1), j, jnp.int32) == 0, m[2], 1.0)
         scale = jnp.sqrt(norm)
@@ -282,27 +298,68 @@
         square = square + 2.0 * alpha * beta_prev * m[5]
         beta = jnp.sqrt(square)
         to_new = 1.0 / (scale * beta)
-        to_here = alpha * to_new
-        to_before = beta_prev / beta
-        to_prev = 1.0 / scale
-        for x in range(0, grid_size, planes):
-            at = slice(SUBLANES * x, SUBLANES * (x + planes))
-            here = vec[at, :]
-            value = to_new * applied[at, :] - to_here * here - to_before * prev[at, :]
-            prev[at, :] = to_prev * here
-            vec[at, :] = value
-            vec_high[at, :], vec_low[at, :] = split(value)
-        alphas = jnp.where(lane == j, alpha, alphas)
-        betas = jnp.where(lane == j, beta, betas)
-        return alphas, betas, beta
-
-    zeros = jnp.zeros((1, LANES), jnp.float32)
-    alphas, betas, _ = lax.fori_loop(0, ITERS, step, (zeros, zeros, jnp.zeros((1, 1), jnp.float32)))
-    coef[0:1, :] = alphas
-    coef[1:2, :] = betas
+        return alpha, beta, to_new, alpha * to_new, beta_prev / beta, 1.0 / scale
+
+    def note(j, alpha, beta, alphas, betas):
+        return jnp.where(lane == j, alpha, alphas), jnp.where(lane == j, beta, betas)
+
+    def step(j, carry):
+        alphas, betas, beta_prev, message = carry
+        grid_total = over_grid(j, message)
+        to_site_and_back()
+        band_total = over_band(j, grid_total())
+        finish_apply(applied, twice)
+        alpha, beta, to_new, to_here, to_before, to_prev = coefficients(j, band_total(), beta_prev)
+
+        def rows_step(r, sums):
+            at = pl.ds(pl.multiple_of(r * tall, tall), tall)
+            for cols in blocks:
+                here, new, before, applied_before = vec[at, cols], applied[at, cols], prev[at, cols], applied_prev[at, cols]
+                vector = to_new * new - to_here * here - to_before * before
+                image = to_new * twice[at, cols] - to_here * new - to_before * applied_before
+                before = to_prev * here
+                vec[at, cols] = vector
+                applied[at, cols] = image
+                prev[at, cols] = before
+                applied_prev[at, cols] = to_prev * new
+                vec_high[at, cols], vec_low[at, cols] = split(image)
+                sums = add_moments(sums, vector, image, before)
+            return sums
+
+        message = message_of(lax.fori_loop(0, rows // tall, rows_step, zero_sums))
+        alphas, betas = note(j, alpha, beta, alphas, betas)
+        return alphas, betas, beta, message
+
+    to_site_and_back()
+    for copy in energy_copies:
+        copy.wait()
     for x in range(grid_size):
         at = slice(SUBLANES * x, SUBLANES * (x + 1))
-        outgoing[x // planes, :, x % planes * cells:(x % planes + 1) * cells] = vec[at, :]
+        energy[at, :] = got_energies[x // planes, :, x % planes * cells:(x % planes + 1) * cells]
+    finish_apply(vec, applied)
+
+    def first_rows(r, sums):
+        at = pl.ds(pl.multiple_of(r * tall, tall), tall)
+        for cols in blocks:
+            here, new = vec[at, cols], applied[at, cols]
+            vec_high[at, cols], vec_low[at, cols] = split(new)
+            sums = add_moments(sums, here, new, jnp.zeros_like(here))
+        return sums
+
+    message = message_of(lax.fori_loop(0, rows // tall, first_rows, zero_sums))
+    zeros = jnp.zeros((1, LANES), jnp.float32)
+    carry = (zeros, zeros, jnp.zeros((1, 1), jnp.float32), message)
+    last = ITERS - 1
+    alphas, betas, beta_prev, message = lax.fori_loop(0, last, step, carry)
+    message = over_band(last, over_grid(last, message)())()
+    alpha, beta, to_new, to_here, to_before, _ = coefficients(last, message, beta_prev)
+    alphas, betas = note(last, alpha, beta, alphas, betas)
+    alphas_out[0] = alphas[:, :ITERS]
+    betas_out[0] = betas[:, :ITERS]
+    for x in range(grid_size):
+        at = slice(SUBLANES * x, SUBLANES * (x + 1))
+        outgoing[x // planes, :, x % planes * cells:(x % planes + 1) * cells] = (
+            to_new * applied[at, :] - to_here * vec[at, :] - to_before * prev[at, :])
     out_copies = []
     for k in range(1, n):
         peer = (me + k) % n
@@ -331,28 +388,30 @@
     x_high = x_wide.astype(jnp.bfloat16)
     x_low = (x_wide - x_high.astype(np.float32)).astype(jnp.bfloat16)
     vmem = pl.BlockSpec(memory_space=pltpu.VMEM)
-    hbm = pl.BlockSpec(memory_space=pl.ANY)
+    hbm = pl.BlockSpec(memory_space=pltpu.MemorySpace.HBM)
     slab = (n, SUBLANES, start.shape[4])
     full = pltpu.VMEM((rows, cells), jnp.float32)
     half = pltpu.VMEM((rows, cells), jnp.bfloat16)
     dma = pltpu.SemaphoreType.DMA
-    out, coef = pl.pallas_call(
+    coef = jax.ShapeDtypeStruct((1, 1, ITERS), jnp.float32)
+    out, alphas, betas = pl.pallas_call(
         functools.partial(recursion_kernel, (n, band_n, grid_size, halves, min(256, cells))),
-        out_shape=(jax.ShapeDtypeStruct(start.shape, jnp.float32), jax.ShapeDtypeStruct((2, LANES), jnp.float32)),
-        in_specs=[hbm, hbm, pl.BlockSpec(memory_space=pltpu.SMEM)] + [vmem] * 5,
-        out_specs=(hbm, vmem),
+        out_shape=(jax.ShapeDtypeStruct(start.shape, jnp.float32), coef, coef),
+        in_specs=[hbm, hbm, pl.BlockSpec(memory_space=pltpu.SMEM)] + [hbm] + [vmem] * 4,
+        out_specs=(pl.BlockSpec(memory_space=pl.ANY), vmem, vmem),
         scratch_shapes=[
+            pltpu.VMEM((grid_size, grid_size, grid_size), jnp.float32), pltpu.VMEM((grid_size, cells), jnp.float32),
             pltpu.VMEM(slab, jnp.float32), pltpu.VMEM(slab, jnp.float32),
-            full, full, full, full, full, half, half, half, half,
+            full, full, full, full, full, full, full, half, half, half, half,
             pltpu.VMEM((cells, cells), jnp.bfloat16), pltpu.VMEM((cells, cells), jnp.bfloat16),
             pltpu.VMEM(slab, jnp.float32),
             pltpu.VMEM((ITERS, n, 1, LANES), jnp.float32), pltpu.VMEM((ITERS, band_n, 1, LANES), jnp.float32),
-            dma((n,)), dma((n,)), dma((n,)), dma((n,)), dma((n,)), dma((n,)),
+            dma(()), dma((n,)), dma((n,)), dma((n,)), dma((n,)), dma((n,)), dma((n,)),
             dma((ITERS, n)), dma((ITERS, n)), dma((ITERS, band_n)), dma((ITERS, band_n)),
         ],
         compiler_params=pltpu.CompilerParams(collective_id=0, has_side_effects=True, vmem_limit_bytes=50 * 1024 * 1024),
-    )(start, energies, sites, potential.reshape(grid_size, cells), y_table, z_table, jnp.asarray(x_high), jnp.asarray(x_low))
-    return coef[0, :ITERS].reshape(1, 1, ITERS), coef[1, :ITERS].reshape(1, 1, ITERS), out
+    )(start, energies, sites[:, 0], potential, y_table, z_table, jnp.asarray(x_high), jnp.asarray(x_low))
+    return alphas, betas, out
 
 
 def body(start, energies, sites, potential):

time: 104 us -> 92.5 us (0.89)
  Pallas kernels: 97.3 us -> 83.1 us
  local copies, waits for them, and re-layouts: 6.02 us -> 8.52 us
    pallas_call x1, Pallas kernels: 97.3 us -> 83.1 us  [field_body(): pl.pallas_call(functools.partial(recursion_kernel, (n, band_n, grid_size,...]
    unnamed x14 -> x17, local copies, waits for them, and re-layouts: 4.17 us -> 8.52 us
    reshape x1 -> x0, local copies, waits for them, and re-layouts: 1.33 us -> none  [field_body(): potential.reshape(grid_size, cells)]
where the time goes in v2:
time: 92.5 us; the launch traced here: 92.3 us
  Pallas kernels  83.1 us (90%)
  local copies, waits for them, and re-layouts  8.52 us (9%)
    pallas_call x1, Pallas kernels, field_body(): pl.pallas_call(functools.partial(recursion_kernel, (n, band_n, grid_size,...  83.1 us
    unnamed x17, local copies, waits for them, and re-layouts  8.52 us

profile of v2, /device:TPU:1, one launch (start us, length us, event | category | flops | bytes accessed | tf_op | source)
XLA Modules:
  0.0 92.3 jit_solution(2002625961323493547)
XLA Ops:
  0.6 0.0 copy-start.6
  0.6 0.6 copy-done.6
  1.3 0.0 copy-start
  1.3 1.2 %copy-done = f32[1,4,1,16,4096]{4,3,2,1,0:T(8,128)S(1)} copy-done((f32[1,4,1,16,4096]{4,3,2,1,0:T(8,128)S(1)}, f32[1,4,1,16,4096]{4,3,2,1,0:T(8,128)}, u32[]{:S(2)}) %copy-start) | copy-done | bytes 1048600
  2.5 0.0 copy-start.1
  2.5 1.0 %copy-done.1 = f32[32,32,32]{2,1,0:T(8,128)S(1)} copy-done((f32[32,32,32]{2,1,0:T(8,128)S(1)}, f32[32,32,32]{2,1,0:T(8,128)}, u32[]{:S(2)}) %copy-start.1) | copy-done | bytes 131096
  3.6 0.0 copy-start.2
  3.6 0.9 copy-done.2
  4.5 0.0 copy-start.3
  4.5 0.9 copy-done.3
  5.4 0.0 copy-start.4
  5.4 0.9 copy-done.4
  6.3 0.0 copy-start.5
  6.3 0.9 copy-done.5
  7.2 83.1 %shard_map.103 = (f32[1,4,1,16,4096]{4,3,2,1,0:T(8,128)S(1)}, f32[1,1,4]{2,1,0:T(1,128)S(1)}, f32[1,1,4]{2,1,0:T(1,128)S(1)}) custom-call(f32[1,4,1,16,4096]{4,3,2,1,0:T(8,128)S(1)} %copy-done, f32[4,16,4096]{2,1,0:T(8,128)} %energies.1, s32[3]{0:T(128)S(1)} %bitcast.1, f32[32,32,32]{2,1,0:T(8,128)S(1)} %copy-done.1, f32[32,1024]{1,0:T(8,128)S(1)} %copy-done.5, ...), custom_call_target="tpu_custom_call" | custom-call | tf_op jit(solution)/shard_map/pallas_call | solution.py:397
  90.3 0.5 copy.14
  90.8 0.5 copy.15
  91.3 1.0 %copy.16 = f32[1,4,1,16,4096]{4,3,2,1,0:T(8,128)} copy(f32[1,4,1,16,4096]{4,3,2,1,0:T(8,128)S(1)} %get-tuple-element.14) | data formatting | bytes 2097152
Async XLA Ops:
  0.6 0.7 copy-start.6
  1.3 1.2 %copy-start = (f32[1,4,1,16,4096]{4,3,2,1,0:T(8,128)S(1)}, f32[1,4,1,16,4096]{4,3,2,1,0:T(8,128)}, u32[]{:S(2)}) copy-start(f32[1,4,1,16,4096]{4,3,2,1,0:T(8,128)} %start.1) | copy-start | bytes 3145732
  2.5 1.0 %copy-start.1 = (f32[32,32,32]{2,1,0:T(8,128)S(1)}, f32[32,32,32]{2,1,0:T(8,128)}, u32[]{:S(2)}) copy-start(f32[32,32,32]{2,1,0:T(8,128)} %pot.1) | copy-start | bytes 393220
  3.6 0.9 copy-start.2
  4.5 0.9 copy-start.3
  5.4 0.9 copy-start.4
  6.3 0.9 copy-start.5

commit v3 on v2

--- a/solution.py
+++ b/solution.py
@@ -121,6 +121,7 @@
 MESH = pl.DeviceIdType.MESH
 LANES = 128
 SUBLANES = 8
+WIDE = 1024
 
 
 def split(value):
@@ -131,9 +132,9 @@
 def dot3(left, right):
     left_high, left_low = left
     right_high, right_low = right
-    total = jnp.dot(left_high, right_high, preferred_element_type=jnp.float32)
-    total += jnp.dot(left_low, right_high, preferred_element_type=jnp.float32)
-    return total + jnp.dot(left_high, right_low, preferred_element_type=jnp.float32)
+    left = jnp.concatenate([left_high, left_low, left_high], axis=1)
+    right = jnp.concatenate([right_high, right_high, right_low], axis=0)
+    return jnp.dot(left, right, preferred_element_type=jnp.float32)
 
 
 def shifted_potential(table, sites, grid_size):
@@ -159,29 +160,32 @@
 
 
 def recursion_kernel(
-    sizes, start, energies, sites, pot, y_table, z_table, x_high, x_low,
-    out, alphas_out, betas_out,
-    pot_here, pot_flat, got, got_energies, vec, prev, applied, applied_prev, twice, energy, site_table, vec_high, vec_low,
-    mid_high, mid_low, mat_high, mat_low, outgoing, grid_sums, band_sums,
-    pot_sem, start_send, start_recv, energy_send, energy_recv, out_send, out_recv,
-    grid_send, grid_recv, band_send, band_recv,
+    sizes, start, energies, sites, pot, y_far, z_far, x_high_far, x_low_far,
+    out, coef,
+    y_table, z_table, x_high, x_low, pot_here, pot_flat, got, got_energies, vec, prev, applied, applied_prev, twice, energy, site_table, vec_high, vec_low,
+    mid_high, mid_low, mat_high, mat_low, outgoing, sums,
+    table_sem, start_send, start_recv, energy_send, energy_recv, out_send, out_recv,
+    sum_send, sum_recv,
 ):
-    n, band_n, grid_size, halves, block = sizes
+    n, band_n, grid_size, halves, block, wide_block = sizes
     me = lax.axis_index("grid")
-    band_me = lax.axis_index("band")
+    rank = lax.axis_index("band") * n + me
     cells = grid_size * grid_size
     planes = grid_size // n
     rows = grid_size * SUBLANES
     total_count = float(rows * cells * n * band_n)
 
-    pot_copy = pltpu.make_async_copy(pot, pot_here, pot_sem)
-    pot_copy.start()
+    table_copies = [
+        pltpu.make_async_copy(source, target, table_sem.at[i])
+        for i, (source, target) in enumerate(((y_far, y_table), (z_far, z_table), (pot, pot_here), (x_high_far, x_high), (x_low_far, x_low)))
+    ]
+    for copy in table_copies:
+        copy.start()
     barrier = pltpu.get_barrier_semaphore()
-    for k in range(1, n):
-        pl.semaphore_signal(barrier, inc=1, device_id={"grid": (me + k) % n}, device_id_type=MESH)
-    for k in range(1, band_n):
-        pl.semaphore_signal(barrier, inc=1, device_id={"band": (band_me + k) % band_n}, device_id_type=MESH)
-    pl.semaphore_wait(barrier, n + band_n - 2)
+    for k in range(1, n * band_n):
+        peer = (rank + k) % (n * band_n)
+        pl.semaphore_signal(barrier, inc=1, device_id={"grid": peer % n, "band": peer // n}, device_id_type=MESH)
+    pl.semaphore_wait(barrier, n * band_n - 1)
 
     def start_piece(owner):
         return start.at[0, owner // halves, 0, pl.ds(pl.multiple_of(owner % halves * SUBLANES, SUBLANES), SUBLANES), :]
@@ -208,6 +212,8 @@
     start_copies = spread(start_piece, got, start_send, start_recv)
     energy_copies = spread(energy_piece, got_energies, energy_send, energy_recv)
 
+    for copy in table_copies:
+        copy.wait()
     def matrix_rows(y, carry):
         high, low = split(y_table[pl.ds(y, 1), :] * z_table[...])
         at = pl.ds(pl.multiple_of(y * grid_size, grid_size), grid_size)
@@ -216,7 +222,6 @@
         return carry
 
     lax.fori_loop(0, grid_size, matrix_rows, 0)
-    pot_copy.wait()
     for y in range(grid_size):
         pot_flat[:, y * grid_size:(y + 1) * grid_size] = pot_here[:, y, :]
     table = shifted_potential(pot_flat[...], sites, grid_size) * (1.0 / (grid_size * cells))
@@ -233,20 +238,21 @@
     vec_high[...], vec_low[...] = split(vec[...])
 
     blocks = [slice(i, i + block) for i in range(0, cells, block)]
+    wide = [slice(i, i + wide_block) for i in range(0, cells, wide_block)]
     lane = lax.broadcasted_iota(jnp.int32, (1, LANES), 1)
     tall = 2 * SUBLANES
     zero_sums = (jnp.zeros((SUBLANES, block), jnp.float32),) * 6
 
     def to_site_and_back():
         x_pair = (x_high[...], x_low[...])
-        for cols in blocks:
+        for cols in wide:
             mat = (mat_high[:, cols], mat_low[:, cols])
             spectrum = dot3((vec_high[...], vec_low[...]), mat)
             spectrum = dot3(x_pair, split(spectrum)) * site_table[:, cols]
             mid_high[:, cols], mid_low[:, cols] = split(dot3(x_pair, split(spectrum)))
 
     def finish_apply(source, target):
-        for cols in blocks:
+        for cols in wide:
             mat = (mat_high[:, cols], mat_low[:, cols])
             target[:, cols] = energy[:, cols] * source[:, cols] - dot3((mid_high[...], mid_low[...]), mat)
 
@@ -254,39 +260,34 @@
         product = a * b
         return product[:SUBLANES] + product[SUBLANES:]
 
-    def add_moments(sums, here, new, before):
+    def add_moments(parts, here, new, before):
         pairs = ((here, new), (new, new), (here, here), (before, before), (before, new), (here, before))
-        return tuple(total + folded(a, b) for total, (a, b) in zip(sums, pairs))
-
-    def message_of(sums):
+        return tuple(total + folded(a, b) for total, (a, b) in zip(parts, pairs))
+
+    def message_of(parts):
         message = jnp.zeros((1, LANES), jnp.float32)
         for i in range(6):
-            value = jnp.sum(jnp.sum(sums[i], axis=0, keepdims=True), axis=1, keepdims=True)
+            value = jnp.sum(jnp.sum(parts[i], axis=0, keepdims=True), axis=1, keepdims=True)
             message = jnp.where(lane == i, value, message)
         return message
 
-    def exchange(j, message, buffer, axis, size, my, send, recv):
-        buffer[j, my] = message
+    def exchange(j, message):
+        sums[j, rank] = message
         copies = []
-        for k in range(1, size):
+        for k in range(1, n * band_n):
+            peer = (rank + k) % (n * band_n)
             copy = pltpu.make_async_remote_copy(
-                src_ref=buffer.at[j, my], dst_ref=buffer.at[j, my], send_sem=send.at[j, k], recv_sem=recv.at[j, k],
-                device_id={axis: (my + k) % size}, device_id_type=MESH)
+                src_ref=sums.at[j, rank], dst_ref=sums.at[j, rank], send_sem=sum_send.at[j, k], recv_sem=sum_recv.at[j, k],
+                device_id={"grid": peer % n, "band": peer // n}, device_id_type=MESH)
             copy.start()
             copies.append(copy)
 
         def total():
             for copy in copies:
                 copy.wait()
-            return jnp.sum(buffer[j], axis=0)
+            return jnp.sum(sums[j], axis=0)
 
         return total
-
-    def over_grid(j, message):
-        return exchange(j, message, grid_sums, "grid", n, me, grid_send, grid_recv)
-
-    def over_band(j, message):
-        return exchange(j, message, band_sums, "band", band_n, band_me, band_send, band_recv)
 
     def coefficients(j, message, beta_prev):
         m = [jnp.sum(jnp.where(lane == i, message, 0.0), axis=1, keepdims=True) / total_count for i in range(6)]
@@ -305,13 +306,12 @@
 
     def step(j, carry):
         alphas, betas, beta_prev, message = carry
-        grid_total = over_grid(j, message)
+        message_total = exchange(j, message)
         to_site_and_back()
-        band_total = over_band(j, grid_total())
         finish_apply(applied, twice)
-        alpha, beta, to_new, to_here, to_before, to_prev = coefficients(j, band_total(), beta_prev)
-
-        def rows_step(r, sums):
+        alpha, beta, to_new, to_here, to_before, to_prev = coefficients(j, message_total(), beta_prev)
+
+        def rows_step(r, parts):
             at = pl.ds(pl.multiple_of(r * tall, tall), tall)
             for cols in blocks:
                 here, new, before, applied_before = vec[at, cols], applied[at, cols], prev[at, cols], applied_prev[at, cols]
@@ -323,8 +323,8 @@
                 prev[at, cols] = before
                 applied_prev[at, cols] = to_prev * new
                 vec_high[at, cols], vec_low[at, cols] = split(image)
-                sums = add_moments(sums, vector, image, before)
-            return sums
+                parts = add_moments(parts, vector, image, before)
+            return parts
 
         message = message_of(lax.fori_loop(0, rows // tall, rows_step, zero_sums))
         alphas, betas = note(j, alpha, beta, alphas, betas)
@@ -338,37 +338,39 @@
         energy[at, :] = got_energies[x // planes, :, x % planes * cells:(x % planes + 1) * cells]
     finish_apply(vec, applied)
 
-    def first_rows(r, sums):
+    def first_rows(r, parts):
         at = pl.ds(pl.multiple_of(r * tall, tall), tall)
         for cols in blocks:
             here, new = vec[at, cols], applied[at, cols]
             vec_high[at, cols], vec_low[at, cols] = split(new)
-            sums = add_moments(sums, here, new, jnp.zeros_like(here))
-        return sums
+            parts = add_moments(parts, here, new, jnp.zeros_like(here))
+        return parts
 
     message = message_of(lax.fori_loop(0, rows // tall, first_rows, zero_sums))
     zeros = jnp.zeros((1, LANES), jnp.float32)
     carry = (zeros, zeros, jnp.zeros((1, 1), jnp.float32), message)
     last = ITERS - 1
     alphas, betas, beta_prev, message = lax.fori_loop(0, last, step, carry)
-    message = over_band(last, over_grid(last, message)())()
+    message = exchange(last, message)()
     alpha, beta, to_new, to_here, to_before, _ = coefficients(last, message, beta_prev)
     alphas, betas = note(last, alpha, beta, alphas, betas)
-    alphas_out[0] = alphas[:, :ITERS]
-    betas_out[0] = betas[:, :ITERS]
-    for x in range(grid_size):
-        at = slice(SUBLANES * x, SUBLANES * (x + 1))
-        outgoing[x // planes, :, x % planes * cells:(x % planes + 1) * cells] = (
-            to_new * applied[at, :] - to_here * vec[at, :] - to_before * prev[at, :])
+    coef[0:1, :] = alphas
+    coef[1:2, :] = betas
     out_copies = []
-    for k in range(1, n):
+    for k in range(1, n + 1):
         peer = (me + k) % n
-        out_copies.append(pltpu.make_async_remote_copy(
-            src_ref=outgoing.at[peer], dst_ref=out_piece(me), send_sem=out_send.at[k], recv_sem=out_recv.at[k],
-            device_id={"grid": peer}, device_id_type=MESH))
-    out_copies.append(pltpu.make_async_copy(outgoing.at[me], out_piece(me), out_send.at[0]))
-    for copy in out_copies:
+        for x in range(planes):
+            at = pl.ds(pl.multiple_of((peer * planes + x) * SUBLANES, SUBLANES), SUBLANES)
+            outgoing[peer, :, x * cells:(x + 1) * cells] = (
+                to_new * applied[at, :] - to_here * vec[at, :] - to_before * prev[at, :])
+        if k < n:
+            copy = pltpu.make_async_remote_copy(
+                src_ref=outgoing.at[peer], dst_ref=out_piece(me), send_sem=out_send.at[k], recv_sem=out_recv.at[k],
+                device_id={"grid": peer}, device_id_type=MESH)
+        else:
+            copy = pltpu.make_async_copy(outgoing.at[me], out_piece(me), out_send.at[0])
         copy.start()
+        out_copies.append(copy)
     for copy in out_copies:
         copy.wait()
 
@@ -393,25 +395,26 @@
     full = pltpu.VMEM((rows, cells), jnp.float32)
     half = pltpu.VMEM((rows, cells), jnp.bfloat16)
     dma = pltpu.SemaphoreType.DMA
-    coef = jax.ShapeDtypeStruct((1, 1, ITERS), jnp.float32)
-    out, alphas, betas = pl.pallas_call(
-        functools.partial(recursion_kernel, (n, band_n, grid_size, halves, min(256, cells))),
-        out_shape=(jax.ShapeDtypeStruct(start.shape, jnp.float32), coef, coef),
-        in_specs=[hbm, hbm, pl.BlockSpec(memory_space=pltpu.SMEM)] + [hbm] + [vmem] * 4,
-        out_specs=(pl.BlockSpec(memory_space=pl.ANY), vmem, vmem),
+    out, coef = pl.pallas_call(
+        functools.partial(recursion_kernel, (n, band_n, grid_size, halves, min(256, cells), min(WIDE, cells))),
+        out_shape=(jax.ShapeDtypeStruct(start.shape, jnp.float32), jax.ShapeDtypeStruct((2, LANES), jnp.float32)),
+        in_specs=[hbm, hbm, pl.BlockSpec(memory_space=pltpu.SMEM)] + [hbm] * 5,
+        out_specs=(vmem, vmem),
         scratch_shapes=[
+            pltpu.VMEM((grid_size, cells), jnp.float32), pltpu.VMEM((grid_size, cells), jnp.float32),
+            pltpu.VMEM((rows, rows), jnp.bfloat16), pltpu.VMEM((rows, rows), jnp.bfloat16),
             pltpu.VMEM((grid_size, grid_size, grid_size), jnp.float32), pltpu.VMEM((grid_size, cells), jnp.float32),
             pltpu.VMEM(slab, jnp.float32), pltpu.VMEM(slab, jnp.float32),
             full, full, full, full, full, full, full, half, half, half, half,
             pltpu.VMEM((cells, cells), jnp.bfloat16), pltpu.VMEM((cells, cells), jnp.bfloat16),
             pltpu.VMEM(slab, jnp.float32),
-            pltpu.VMEM((ITERS, n, 1, LANES), jnp.float32), pltpu.VMEM((ITERS, band_n, 1, LANES), jnp.float32),
-            dma(()), dma((n,)), dma((n,)), dma((n,)), dma((n,)), dma((n,)), dma((n,)),
-            dma((ITERS, n)), dma((ITERS, n)), dma((ITERS, band_n)), dma((ITERS, band_n)),
+            pltpu.VMEM((ITERS, n * band_n, 1, LANES), jnp.float32),
+            dma((5,)), dma((n,)), dma((n,)), dma((n,)), dma((n,)), dma((n,)), dma((n,)),
+            dma((ITERS, n * band_n)), dma((ITERS, n * band_n)),
         ],
-        compiler_params=pltpu.CompilerParams(collective_id=0, has_side_effects=True, vmem_limit_bytes=50 * 1024 * 1024),
+        compiler_params=pltpu.CompilerParams(collective_id=0, has_side_effects=True, vmem_limit_bytes=60 * 1024 * 1024),
     )(start, energies, sites[:, 0], potential, y_table, z_table, jnp.asarray(x_high), jnp.asarray(x_low))
-    return alphas, betas, out
+    return coef[0, :ITERS].reshape(1, 1, ITERS), coef[1, :ITERS].reshape(1, 1, ITERS), out
 
 
 def body(start, energies, sites, potential):

time: 92.5 us -> 76.4 us (0.83)
  Pallas kernels: 83.1 us -> 72.1 us
  local copies, waits for them, and re-layouts: 8.52 us -> 3.45 us
    pallas_call x1, Pallas kernels: 83.1 us -> 72.1 us  [field_body(): pl.pallas_call(functools.partial(recursion_kernel, (n, band_n, grid_size,...]
    unnamed x17 -> x3, local copies, waits for them, and re-layouts: 8.52 us -> 2.93 us
where the time goes in v3:
time: 76.4 us; the launch traced here: 76.2 us
  Pallas kernels  72.1 us (94%)
  local copies, waits for them, and re-layouts  3.45 us (5%)
    pallas_call x1, Pallas kernels, field_body(): pl.pallas_call(functools.partial(recursion_kernel, (n, band_n, grid_size,...  72.1 us
    unnamed x3, local copies, waits for them, and re-layouts  2.93 us

profile of v3, /device:TPU:1, one launch (start us, length us, event | category | flops | bytes accessed | tf_op | source)
XLA Modules:
  0.0 76.2 jit_solution(15799455582278026090)
XLA Ops:
  0.6 72.1 %shard_map.103 = (f32[1,4,1,16,4096]{4,3,2,1,0:T(8,128)}, f32[2,128]{1,0:T(2,128)}) custom-call(f32[1,4,1,16,4096]{4,3,2,1,0:T(8,128)} %start.1, f32[4,16,4096]{2,1,0:T(8,128)} %energies.1, s32[3]{0:T(128)} %bitcast.5, f32[32,32,32]{2,1,0:T(8,128)} %pot.1, f32[32,1024]{1,0:T(8,128)} %constant.8.clone.y_far, f32[32,1024]{1,0:T(8,128)} %constant.9.clone.z_far, ...), custom_call_target="tpu_custom_call" | custom-call | tf_op jit(solution)/shard_map/pallas_call | solution.py:398
  72.8 0.0 copy-start
  72.8 0.7 copy-done
  73.4 0.5 slice_bitcast_fusion
  74.0 2.3 %copy.12 = f32[1,4,1,16,4096]{4,3,2,1,0:T(8,128)} copy(f32[1,4,1,16,4096]{4,3,2,1,0:T(8,128)} %get-tuple-element.14) | data formatting | bytes 2097152
Async XLA Ops:
  72.8 0.7 copy-start
